TPU v7x, 32 devices: a whole 2x2x4 slice. The times are simulated.
32 devices in a mesh: grp: 4 (over y, x), dom: 8 (over z, core).
Axes of the slice: x: 2, y: 2, z: 4, core: 2. Of those that a mesh axis runs over, the one named last changes fastest.
Arguments:
- fields: float32 [210, 32768], P(None, ('grp', 'dom')), may hold values from -6 to 6
- metric: float32 [9, 32768], P(None, ('grp', 'dom')), may hold values from -5 to 5
- normals: float32 [12, 32768], P(None, ('grp', 'dom')), may hold values from -3 to 3
- fscale: float32 [4, 32768], P(None, ('grp', 'dom')), may hold values from 0.5 to 4
- orders: int32 [32768], P(('grp', 'dom')), may hold values from 1 to 4, as said below
- slots: int32 [32768], P(('grp', 'dom')), may hold values from 0 to 511, as said below
- send_faces: int32 [294912], P(('grp', 'dom')), may hold values from 0 to 8192, as said below
- recv_faces: int32 [262144], P(('grp', 'dom')), may hold values from 0 to 9216, as said below
- dmat: float32 [4, 105, 35], P('grp'), may hold values from -4 to 4
- tmat: float32 [4, 60, 35], P('grp'), may hold values from -4 to 4
- lmat: float32 [4, 35, 60], P('grp'), may hold values from -3 to 3
Outputs:
- rhs: float32 [210, 65536], P(None, ('grp', 'dom'))
Inputs may be any that keep to these rules, and one draw needn't show every extreme that they name: `orders`: on each device every order from 1 to 4 is held by at least one element and by at most 512; one order is held by exactly 512. The elements of one device that share an order have distinct slots. `send_faces`: each entry names a face of an occupied slot of the sending bucket or equals 4 * 2048 (nothing); in each list the items in use stand first. `recv_faces`: every face of an occupied slot names a distinct received item that is in use, and every item in use is named by exactly one face; faces of empty slots hold 9216. A list carries at most 768 items in use, and some list carries exactly 768.
All inputs are finite; a program needn't handle non-finite values.
Results may differ from a plain program's by a relative error of at most 0.0003.
Values sent between devices are 32-bit elements; how exact they have to be, the bound alone decides.
A program may use at most 128 MiB of HBM per device.

v0:
```python
import jax
import jax.numpy as jnp
from jax import lax
from jax.sharding import PartitionSpec as P

NPM = 35
FPTS = 15


exact_prec = lax.Precision.HIGHEST


def shifted(x, axis, by):
    size = lax.axis_size(axis)
    return lax.ppermute(x, axis, [(i, (i + by) % size) for i in range(size)])


def order_mask(order_index):
    node_total = (order_index + 2) * (order_index + 3) * (order_index + 4) // 6
    return (jnp.arange(NPM, dtype=jnp.int32) < node_total).astype(jnp.float32)


def cross_of(first_vec, second_vec):
    return [
        first_vec[1] * second_vec[2] - first_vec[2] * second_vec[1],
        first_vec[2] * second_vec[0] - first_vec[0] * second_vec[2],
        first_vec[0] * second_vec[1] - first_vec[1] * second_vec[0],
    ]


def volume_terms(coefficients, metric_cols, deriv_mats):
    derived = jnp.einsum("anm,qms->qans", deriv_mats, coefficients, precision=exact_prec)

    def partial_of(component, direction):
        return (
            metric_cols[0, direction][None] * derived[component, 0]
            + metric_cols[1, direction][None] * derived[component, 1]
            + metric_cols[2, direction][None] * derived[component, 2]
        )

    curl_h = [
        partial_of(5, 1) - partial_of(4, 2),
        partial_of(3, 2) - partial_of(5, 0),
        partial_of(4, 0) - partial_of(3, 1),
    ]
    curl_e = [
        partial_of(2, 1) - partial_of(1, 2),
        partial_of(0, 2) - partial_of(2, 0),
        partial_of(1, 0) - partial_of(0, 1),
    ]
    return jnp.stack(curl_h + [-value for value in curl_e], 0)


def face_flux(own_traces, neighbour, normal_cols, scale_cols):
    own_split = own_traces.reshape(6, FPTS, -1)
    far_split = neighbour.reshape(6, FPTS, -1)
    jump_e = [far_split[c] - own_split[c] for c in range(3)]
    jump_h = [far_split[c + 3] - own_split[c + 3] for c in range(3)]
    normal = [normal_cols[c] for c in range(3)]
    normal_e = normal[0] * jump_e[0] + normal[1] * jump_e[1] + normal[2] * jump_e[2]
    normal_h = normal[0] * jump_h[0] + normal[1] * jump_h[1] + normal[2] * jump_h[2]
    turn_h = cross_of(normal, jump_h)
    turn_e = cross_of(normal, jump_e)
    flux_e = [0.5 * scale_cols * (turn_h[c] + jump_e[c] - normal[c] * normal_e) for c in range(3)]
    flux_h = [0.5 * scale_cols * (-turn_e[c] + jump_h[c] - normal[c] * normal_h) for c in range(3)]
    return jnp.stack(flux_e + flux_h, 0)


def block_rhs(bucket, own_traces, neighbour, deriv_mats, lift_mat):
    slot_count = bucket.shape[1]
    coefficients = bucket[: 6 * NPM].reshape(6, NPM, slot_count)
    metric_cols = bucket[6 * NPM : 6 * NPM + 9].reshape(3, 3, slot_count)
    normal_cols = bucket[6 * NPM + 9 : 6 * NPM + 21].reshape(3, 1, 4 * slot_count)
    scale_cols = bucket[6 * NPM + 21 : 6 * NPM + 25].reshape(1, 4 * slot_count)
    volume = volume_terms(coefficients, metric_cols, deriv_mats)
    flux = face_flux(own_traces, neighbour, normal_cols, scale_cols).reshape(
        6, FPTS * 4, slot_count
    )
    lifted = jnp.einsum("mp,qps->qms", lift_mat, flux, precision=exact_prec)
    return (volume + lifted).reshape(6 * NPM, slot_count)


def across_groups(outgoing):
    return lax.all_to_all(outgoing, "grp", split_axis=1, concat_axis=1, tiled=True)


def across_columns(outgoing):
    lowered = shifted(outgoing[0], "dom", -1)
    raised = shifted(outgoing[2], "dom", 1)
    return jnp.stack([lowered, outgoing[1], raised], 0)


def local(fields, metric, normals, fscale, orders, slots, send_faces, recv_faces, dmat, tmat, lmat):
    own_group = lax.axis_index("grp")
    groups = lax.axis_size("grp")
    elements = fields.shape[1]
    capacity = elements // 2
    slot_count = groups * capacity
    payload = jnp.concatenate([fields, metric, normals, fscale], 0)
    row_count = payload.shape[0]
    zero_column = jnp.zeros((row_count, 1), jnp.float32)
    target = (orders - 1) * capacity + slots
    inverse = (
        jnp.full((slot_count,), elements, jnp.int32)
        .at[target]
        .set(jnp.arange(elements, dtype=jnp.int32))
    )
    padded = jnp.concatenate([payload, zero_column], 1)
    outgoing = jnp.take(padded, inverse, axis=1).reshape(row_count, groups, capacity)
    bucket = lax.all_to_all(outgoing, "grp", split_axis=1, concat_axis=1, tiled=True).reshape(
        row_count, slot_count
    )
    node_mask = order_mask(own_group)
    deriv_mats = dmat[0].reshape(3, NPM, NPM) * node_mask[None, :, None] * node_mask[None, None, :]
    trace_mat = tmat[0] * node_mask[None, :]
    lift_mat = lmat[0] * node_mask[:, None]
    coefficients = bucket[: 6 * NPM].reshape(6, NPM, slot_count)
    own_traces = jnp.einsum("pm,qms->qps", trace_mat, coefficients, precision=exact_prec).reshape(
        6 * FPTS, 4 * slot_count
    )
    face_rows = jnp.concatenate([own_traces.T, jnp.zeros((1, 6 * FPTS), jnp.float32)], 0)
    list_total = send_faces.shape[0]
    list_size = list_total // (3 * groups)
    outgoing_faces = jnp.take(face_rows, send_faces, axis=0).reshape(3, groups, list_size, 6 * FPTS)
    arrived = across_columns(across_groups(outgoing_faces))
    received = jnp.concatenate(
        [arrived.reshape(list_total, 6 * FPTS), jnp.zeros((1, 6 * FPTS), jnp.float32)], 0
    )
    neighbour = jnp.take(received, recv_faces, axis=0).T
    return block_rhs(bucket, own_traces, neighbour, deriv_mats, lift_mat)


def solution(mesh):
    in_specs = (
        P(None, ("grp", "dom")),
        P(None, ("grp", "dom")),
        P(None, ("grp", "dom")),
        P(None, ("grp", "dom")),
        P(("grp", "dom")),
        P(("grp", "dom")),
        P(("grp", "dom")),
        P(("grp", "dom")),
        P("grp", None, None),
        P("grp", None, None),
        P("grp", None, None),
    )
    out_specs = P(None, ("grp", "dom"))
    return jax.shard_map(local, mesh=mesh, in_specs=in_specs, out_specs=out_specs, check_vma=False)
```

profile of v0, /device:TPU:1, one launch (start us, length us, event | category | flops | bytes accessed | tf_op | source)
XLA Modules:
  0.0 281.7 jit_solution(4036362159378918942)
XLA Ops:
  0.7 4.3 %scatter_custom_fusion = s32[2048]{0:T(1024)S(1)} fusion(s32[1024]{0:T(1024)S(1)} %compare_select_fusion.3, s32[1024]{0:T(1024)S(1)} %iota.14, s32[]{:T(128)} %constant.33.clone.1), kind=kCustom, calls=%fused_computation.79 | custom fusion | bytes 8196 | tf_op jit(solution)/shard_map/scatter | solution.py:106
  11.3 6.6 %gather_fusion = f32[2048,235]{1,0:T(8,128)S(1)} fusion(f32[235,1025]{0,1:T(8,128)S(1)} %select_maximum_fusion, s32[2048]{0:T(1024)S(1)} %fusion.11), kind=kCustom, calls=%fused_computation | custom fusion | bytes 3858432 | tf_op jit(solution)/shard_map/jit(_take)/gather | solution.py:109
  19.8 3.1 %broadcast_select_fusion.1 = f32[235,4,512]{2,0,1:T(8,128)} fusion(f32[235,4,512]{2,0,1:T(8,128)} %copy.62, pred[4,512]{1,0:T(4,128)(4,1)S(1)} %broadcast_in_dim.53), kind=kLoop, calls=%fused_computation.20 | loop fusion | flops 481280 | bytes 3852288 | tf_op jit(solution)/shard_map/jit(_take)/select_n | solution.py:109
  22.9 4.4 %all-to-all-start = ((f32[235,4,512]{2,0,1:T(8,128)}), f32[235,4,512]{2,0,1:T(8,128)S(1)}, u32[]{:S(2)}, u32[]{:S(2)}) async-start(f32[235,4,512]{2,0,1:T(8,128)} %broadcast_select_fusion.1), calls=%async_computation | async-start | bytes 3932160 | tf_op jit(solution)/shard_map/all_to_all | solution.py:110
  29.8 20.6 %all-to-all-done = f32[235,4,512]{2,0,1:T(8,128)S(1)} async-done(((f32[235,4,512]{2,0,1:T(8,128)}), f32[235,4,512]{2,0,1:T(8,128)S(1)}, u32[]{:S(2)}, u32[]{:S(2)}) %all-to-all-start) | async-done | bytes 1925152 | tf_op jit(solution)/shard_map/all_to_all | solution.py:110
  52.9 2.5 reshape.2020
  55.4 2.6 reshape.2060
  58.0 4.7 %convolution_bitcast_fusion.1 = f32[6,60,2048]{2,1,0:T(8,128)S(1)} fusion(f32[6,35,2048]{2,1,0:T(8,128)} %reshape.2020, f32[1,60,35]{1,0,2:T(1,128)S(1)} %broadcast_multiply_fusion), kind=kOutput, calls=%fused_computation.7 | convolution fusion | flops 309657600 | bytes 4677840 | tf_op jit(solution)/shard_map/pm,qms->qps/dot_general | solution.py:118
  62.7 3.0 %reshape.2021 = f32[90,8192]{1,0:T(8,128)} reshape(f32[6,60,2048]{2,1,0:T(8,128)S(1)} %convolution_bitcast_fusion.1) | data formatting | bytes 5898240 | tf_op jit(solution)/shard_map/reshape | solution.py:118
  65.7 5.2 %copy.67 = f32[90,8192]{0,1:T(8,128)} copy(f32[90,8192]{1,0:T(8,128)} %reshape.2021) | data formatting | bytes 5898240 | tf_op jit(solution)/shard_map/reshape | solution.py:118
  70.8 3.8 %concatenate.15 = f32[8193,90]{1,0:T(8,128)} pad(f32[8192,90]{1,0:T(8,128)} %bitcast.170, f32[]{:T(128)} %constant.45.clone.1), padding=0_1x0_0 | pad | bytes 5898604 | tf_op jit(solution)/shard_map/concatenate | solution.py:121
  74.6 33.3 %gather_fusion.1 = f32[9216,90]{1,0:T(8,128)} fusion(f32[8193,90]{1,0:T(8,128)} %concatenate.15, s32[9216]{0:T(1024)S(1)} %fusion.3), kind=kCustom, calls=%fused_computation.1 | custom fusion | bytes 6672384 | tf_op jit(solution)/shard_map/jit(_take)/gather | solution.py:124
  107.9 3.9 %copy.68 = f32[3,4,768,90]{2,3,0,1:T(8,128)S(1)} copy(f32[3,4,768,90]{3,2,1,0:T(8,128)} %bitcast.168) | data formatting | bytes 6635520 | tf_op jit(solution)/shard_map/jit(_take)/gather | solution.py:124
  114.1 4.0 %all-to-all-start.1 = ((f32[3,4,768,90]{2,3,0,1:T(8,128)}), f32[3,4,768,90]{2,3,0,1:T(8,128)S(1)}, u32[]{:S(2)}, u32[]{:S(2)}) async-start(f32[3,4,768,90]{2,3,0,1:T(8,128)} %broadcast_select_fusion), calls=%async_computation.1 | async-start | bytes 7077888 | tf_op jit(solution)/shard_map/all_to_all | solution.py:84
  118.0 10.5 %convolution_bitcast_fusion = f32[6,3,35,2048]{3,2,1,0:T(8,128)} fusion(f32[6,35,2048,1]{2,1,0,3:T(8,128)} %reshape.2060, f32[3,35,35]{2,1,0:T(8,128)} %copy.65), kind=kOutput, calls=%fused_computation.5 | convolution fusion | flops 541900800 | bytes 6895980 | tf_op jit(solution)/shard_map/anm,qms->qans/dot_general | solution.py:32
  142.4 15.2 %all-to-all-done.1 = f32[3,4,768,90]{2,3,0,1:T(8,128)S(1)} async-done(((f32[3,4,768,90]{2,3,0,1:T(8,128)}), f32[3,4,768,90]{2,3,0,1:T(8,128)S(1)}, u32[]{:S(2)}, u32[]{:S(2)}) %all-to-all-start.1) | async-done | bytes 3317792 | tf_op jit(solution)/shard_map/all_to_all | solution.py:84
  159.5 2.7 collective-permute-start.1
  174.3 7.7 %collective-permute-done.1 = f32[4,768,90]{1,0,2:T(4,128)S(1)} collective-permute-done((f32[4,768,90]{1,0,2:T(4,128)S(1)}, f32[4,768,90]{1,0,2:T(4,128)S(1)}, u32[]{:S(2)}, u32[]{:S(2)}) %collective-permute-start.1) | collective-permute-done | bytes 1105952 | tf_op jit(solution)/shard_map/ppermute | solution.py:15
  182.3 6.7 %collective-permute-done = f32[4,768,90]{1,0,2:T(4,128)} collective-permute-done((f32[4,768,90]{1,0,2:T(4,128)}, f32[4,768,90]{1,0,2:T(4,128)}, u32[]{:S(2)}, u32[]{:S(2)}) %collective-permute-start) | collective-permute-done | bytes 1105952 | tf_op jit(solution)/shard_map/ppermute | solution.py:15
  190.7 3.6 %copy.73 = f32[3,4,768,90]{3,2,1,0:T(8,128)} copy(f32[3,4,768,90]{2,3,0,1:T(8,128)S(1)} %pad_maximum_fusion) | data formatting | bytes 6635520 | tf_op jit(solution)/shard_map/stack | solution.py:90
  194.3 4.0 %concatenate.16 = f32[9217,90]{1,0:T(8,128)} pad(f32[9216,90]{1,0:T(8,128)} %bitcast.169, f32[]{:T(128)} %constant.45.clone.1), padding=0_1x0_0 | pad | bytes 6635884 | tf_op jit(solution)/shard_map/concatenate | solution.py:126
  198.3 30.1 %gather_fusion.2 = f32[8192,90]{1,0:T(8,128)} fusion(f32[9217,90]{1,0:T(8,128)} %concatenate.16, s32[8192]{0:T(1024)S(1)} %copy-done.25), kind=kCustom, calls=%fused_computation.2 | custom fusion | bytes 5931008 | tf_op jit(solution)/shard_map/jit(_take)/gather | solution.py:129
  228.4 6.2 %select_bitcast_fusion = f32[90,8192]{0,1:T(8,128)S(1)} fusion(f32[8192,90]{1,0:T(8,128)} %gather_fusion.2, pred[8192]{0:T(1024)(128)(4,1)S(1)} %copy-done.26), kind=kLoop, calls=%fused_computation.4 | loop fusion | flops 737280 | bytes 5906432 | tf_op jit(solution)/shard_map/jit(_take)/select_n | solution.py:129
  234.6 11.1 %fusion.14 = (f32[15,8192]{0,1:T(8,128)}, f32[15,8192]{0,1:T(8,128)}, f32[15,8192]{0,1:T(8,128)}, f32[15,8192]{0,1:T(8,128)}, f32[15,8192]{0,1:T(8,128)}, /*index=5*/f32[15,8192]{0,1:T(8,128)}) fusion(f32[90,8192]{0,1:T(8,128)S(1)} %select_bitcast_fusion), kind=kLoop, calls=%fused_computation.82 | loop fusion | bytes 5898240 | tf_op jit(solution)/shard_map/slice | solution.py:58
  245.7 2.8 %copy.74 = f32[15,8192]{1,0:T(8,128)S(1)} copy(f32[15,8192]{0,1:T(8,128)} %get-tuple-element.18) | data formatting | bytes 983040 | tf_op jit(solution)/shard_map/slice | solution.py:58
  249.5 2.8 %copy.75 = f32[15,8192]{1,0:T(8,128)S(1)} copy(f32[15,8192]{0,1:T(8,128)} %get-tuple-element.17) | data formatting | bytes 983040 | tf_op jit(solution)/shard_map/slice | solution.py:58
  253.3 2.8 %copy.76 = f32[15,8192]{1,0:T(8,128)S(1)} copy(f32[15,8192]{0,1:T(8,128)} %get-tuple-element.16) | data formatting | bytes 983040 | tf_op jit(solution)/shard_map/slice | solution.py:57
  257.1 2.8 %copy.77 = f32[15,8192]{1,0:T(8,128)S(1)} copy(f32[15,8192]{0,1:T(8,128)} %get-tuple-element.15) | data formatting | bytes 983040 | tf_op jit(solution)/shard_map/slice | solution.py:57
  260.9 2.8 %copy.78 = f32[15,8192]{1,0:T(8,128)S(1)} copy(f32[15,8192]{0,1:T(8,128)} %get-tuple-element.14) | data formatting | bytes 983040 | tf_op jit(solution)/shard_map/slice | solution.py:57
  264.7 3.7 %copy.79 = f32[15,8192]{1,0:T(8,128)} copy(f32[15,8192]{0,1:T(8,128)} %get-tuple-element.13) | data formatting | bytes 983040 | tf_op jit(solution)/shard_map/slice | solution.py:58
  270.4 3.2 %multiply_dynamic-update-slice_fusion.5 = (f32[6,60,2048]{2,1,0:T(8,128)S(1)}, f32[1,60,2048]{2,1,0:T(8,128)S(1)}, f32[1,60,2048]{2,1,0:T(8,128)S(1)}, f32[1,60,...) fusion(f32[1,60,2048]{2,1,0:T(8,128)} %mul.929, f32[1,60,2048]{2,1,0:T(8,128)} %mul.943, ...), kind=kLoop, calls=%fused_computation.33 | loop fusion | flops 2088959 | bytes 10027008
  276.1 4.2 %fusion = f32[6,35,2048]{2,1,0:T(8,128)S(1)} fusion(f32[6,35,2048]{2,1,0:T(8,128)} %negate_dynamic-update-slice_fusion, f32[6,60,2048]{2,1,0:T(8,128)S(1)} %multiply_dynamic-update-slice_fusion, f32[1,35,60]{2,0,1:T(1,128)S(1)} %copy-done.27, f32[35]{0:T(128)S(1)} %copy-done.32), kind=kOutput, calls=%fused_computation.9 | convolution fusion | flops 310089792 | bytes 6398300 | tf_op jit(solution)/shard_map/mp,qps->qms/dot_general | solution.py:79
  (131 shorter events, 56.2 us)
Async XLA Ops:
  0.0 8.7 %copy-start.30 = (f32[4,1024]{1,0:T(4,128)S(1)}, f32[4,1024]{1,0:T(4,128)}, u32[]{:S(2)}) copy-start(f32[4,1024]{1,0:T(4,128)} %param.14) | copy-start | bytes 49156
  19.7 7.6 %copy-start.23 = (s32[9216]{0:T(1024)S(1)}, s32[9216]{0:T(1024)}, u32[]{:S(2)}) copy-start(s32[9216]{0:T(1024)} %param.17) | copy-start | bytes 110596
  19.7 7.8 %copy-start.28 = (f32[1,105,35]{1,0,2:T(1,128)S(1)}, f32[1,105,35]{1,0,2:T(1,128)}, u32[]{:S(2)}) copy-start(f32[1,105,35]{1,0,2:T(1,128)} %param.19) | copy-start | bytes 44104
  19.8 8.7 %copy-start.29 = (f32[1,60,35]{1,0,2:T(1,128)S(1)}, f32[1,60,35]{1,0,2:T(1,128)}, u32[]{:S(2)}) copy-start(f32[1,60,35]{1,0,2:T(1,128)} %param.20) | copy-start | bytes 25204
  22.9 5.7 %copy-start.24 = (s32[8192]{0:T(1024)S(1)}, s32[8192]{0:T(1024)}, u32[]{:S(2)}) copy-start(s32[8192]{0:T(1024)} %param.18) | copy-start | bytes 98308
  22.9 27.5 %all-to-all-start = ((f32[235,4,512]{2,0,1:T(8,128)}), f32[235,4,512]{2,0,1:T(8,128)S(1)}, u32[]{:S(2)}, u32[]{:S(2)}) async-start(f32[235,4,512]{2,0,1:T(8,128)} %broadcast_select_fusion.1), calls=%async_computation | async-start | bytes 3932160 | tf_op jit(solution)/shard_map/all_to_all | solution.py:110
  27.4 25.5 %copy-start.31 = (f32[35]{0:T(128)}, f32[35]{0:T(128)S(1)}, u32[]{:S(2)}) copy-start(f32[35]{0:T(128)S(1)} %compare_convert_fusion) | copy-start | bytes 424
  114.1 43.5 %all-to-all-start.1 = ((f32[3,4,768,90]{2,3,0,1:T(8,128)}), f32[3,4,768,90]{2,3,0,1:T(8,128)S(1)}, u32[]{:S(2)}, u32[]{:S(2)}) async-start(f32[3,4,768,90]{2,3,0,1:T(8,128)} %broadcast_select_fusion), calls=%async_computation.1 | async-start | bytes 7077888 | tf_op jit(solution)/shard_map/all_to_all | solution.py:84
  132.8 7.2 %copy-start.9 = (f32[1,1,2048]{2,1,0:T(1,128)}, f32[1,1,2048]{2,1,0:T(1,128)S(1)}, u32[]{:S(2)}) copy-start(f32[1,1,2048]{2,1,0:T(1,128)S(1)} %get-tuple-element.28) | copy-start | bytes 24580
  132.8 7.2 %copy-start.11 = (f32[1,1,2048]{2,1,0:T(1,128)}, f32[1,1,2048]{2,1,0:T(1,128)S(1)}, u32[]{:S(2)}) copy-start(f32[1,1,2048]{2,1,0:T(1,128)S(1)} %get-tuple-element.32) | copy-start | bytes 24580
  132.8 7.2 %copy-start.13 = (f32[1,1,2048]{2,1,0:T(1,128)}, f32[1,1,2048]{2,1,0:T(1,128)S(1)}, u32[]{:S(2)}) copy-start(f32[1,1,2048]{2,1,0:T(1,128)S(1)} %get-tuple-element.33) | copy-start | bytes 24580
  132.8 7.2 %copy-start.15 = (f32[1,1,2048]{2,1,0:T(1,128)}, f32[1,1,2048]{2,1,0:T(1,128)S(1)}, u32[]{:S(2)}) copy-start(f32[1,1,2048]{2,1,0:T(1,128)S(1)} %get-tuple-element.34) | copy-start | bytes 24580
  132.8 7.2 %copy-start.17 = (f32[1,1,2048]{2,1,0:T(1,128)}, f32[1,1,2048]{2,1,0:T(1,128)S(1)}, u32[]{:S(2)}) copy-start(f32[1,1,2048]{2,1,0:T(1,128)S(1)} %get-tuple-element.29) | copy-start | bytes 24580
  132.8 7.2 %copy-start.19 = (f32[1,1,2048]{2,1,0:T(1,128)}, f32[1,1,2048]{2,1,0:T(1,128)S(1)}, u32[]{:S(2)}) copy-start(f32[1,1,2048]{2,1,0:T(1,128)S(1)} %get-tuple-element.30) | copy-start | bytes 24580
  132.8 7.2 %copy-start.21 = (f32[1,1,2048]{2,1,0:T(1,128)}, f32[1,1,2048]{2,1,0:T(1,128)S(1)}, u32[]{:S(2)}) copy-start(f32[1,1,2048]{2,1,0:T(1,128)S(1)} %get-tuple-element.31) | copy-start | bytes 24580
  159.5 22.5 %collective-permute-start.1 = (f32[4,768,90]{1,0,2:T(4,128)S(1)}, f32[4,768,90]{1,0,2:T(4,128)S(1)}, u32[]{:S(2)}, u32[]{:S(2)}) collective-permute-start(f32[4,768,90]{1,0,2:T(4,128)S(1)} %copy.71), channel_id=1, source_target_pairs={{0,1},{1,2},{2,3},{3,4},{4,5},{5,6},{6,7},{7,0},{8,9},{9,10},{10,1... | collective-permute-start | bytes 3317768 | tf_op jit(solution)/shard_map/ppermute | solution.py:15
  164.0 25.0 %collective-permute-start = (f32[4,768,90]{1,0,2:T(4,128)}, f32[4,768,90]{1,0,2:T(4,128)}, u32[]{:S(2)}, u32[]{:S(2)}) collective-permute-start(f32[4,768,90]{1,0,2:T(4,128)} %copy.69), channel_id=1, source_target_pairs={{0,7},{1,0},{2,1},{3,2},{4,3},{5,4},{6,5},{7,6},{8,15},{9,8},{10,9... | collective-permute-start | bytes 3317768 | tf_op jit(solution)/shard_map/ppermute | solution.py:15
  165.1 4.4 %copy-start.10 = (f32[1,1,2048]{2,1,0:T(1,128)S(1)}, f32[1,1,2048]{2,1,0:T(1,128)}, u32[]{:S(2)}) copy-start(f32[1,1,2048]{2,1,0:T(1,128)} %copy-done.9) | copy-start | bytes 24580
  165.1 4.4 %copy-start.18 = (f32[1,1,2048]{2,1,0:T(1,128)S(1)}, f32[1,1,2048]{2,1,0:T(1,128)}, u32[]{:S(2)}) copy-start(f32[1,1,2048]{2,1,0:T(1,128)} %copy-done.17) | copy-start | bytes 24580
  165.1 4.4 %copy-start.20 = (f32[1,1,2048]{2,1,0:T(1,128)S(1)}, f32[1,1,2048]{2,1,0:T(1,128)}, u32[]{:S(2)}) copy-start(f32[1,1,2048]{2,1,0:T(1,128)} %copy-done.19) | copy-start | bytes 24580
  165.1 4.4 %copy-start.22 = (f32[1,1,2048]{2,1,0:T(1,128)S(1)}, f32[1,1,2048]{2,1,0:T(1,128)}, u32[]{:S(2)}) copy-start(f32[1,1,2048]{2,1,0:T(1,128)} %copy-done.21) | copy-start | bytes 24580
  166.3 5.6 %copy-start.12 = (f32[1,1,2048]{2,1,0:T(1,128)S(1)}, f32[1,1,2048]{2,1,0:T(1,128)}, u32[]{:S(2)}) copy-start(f32[1,1,2048]{2,1,0:T(1,128)} %copy-done.11) | copy-start | bytes 24580
  166.3 5.6 %copy-start.14 = (f32[1,1,2048]{2,1,0:T(1,128)S(1)}, f32[1,1,2048]{2,1,0:T(1,128)}, u32[]{:S(2)}) copy-start(f32[1,1,2048]{2,1,0:T(1,128)} %copy-done.13) | copy-start | bytes 24580
  166.3 5.6 %copy-start.16 = (f32[1,1,2048]{2,1,0:T(1,128)S(1)}, f32[1,1,2048]{2,1,0:T(1,128)}, u32[]{:S(2)}) copy-start(f32[1,1,2048]{2,1,0:T(1,128)} %copy-done.15) | copy-start | bytes 24580
  171.8 18.6 %copy-start.7 = (f32[1,4,768,90]{2,3,0,1:T(8,128)S(1)}, f32[1,4,768,90]{2,3,0,1:T(8,128)}, u32[]{:S(2)}) copy-start(f32[1,4,768,90]{2,3,0,1:T(8,128)} %get-tuple-element.21) | copy-start | bytes 3317764
  194.3 4.0 %copy-start.25 = (s32[8192]{0:T(1024)S(1)}, s32[8192]{0:T(1024)}, u32[]{:S(2)}) copy-start(s32[8192]{0:T(1024)} %fusion.4) | copy-start | bytes 98308
  198.3 30.1 %copy-start.26 = (pred[8192]{0:T(1024)(128)(4,1)S(1)}, pred[8192]{0:T(1024)(128)(4,1)}, u32[]{:S(2)}) copy-start(pred[8192]{0:T(1024)(128)(4,1)} %compare_and_fusion.1) | copy-start | bytes 24580
  264.7 5.7 %copy-start.1 = (f32[6,60,2048]{2,1,0:T(8,128)S(1)}, f32[6,60,2048]{2,1,0:T(8,128)}, u32[]{:S(2)}) copy-start(f32[6,60,2048]{2,1,0:T(8,128)} %copy-done) | copy-start | bytes 8847364
  270.4 3.2 %copy-start.3 = (f32[1,60,2048]{2,1,0:T(8,128)S(1)}, f32[1,60,2048]{2,1,0:T(8,128)}, u32[]{:S(2)}) copy-start(f32[1,60,2048]{2,1,0:T(8,128)} %mul.932) | copy-start | bytes 1474564
  270.4 3.2 %copy-start.4 = (f32[1,60,2048]{2,1,0:T(8,128)S(1)}, f32[1,60,2048]{2,1,0:T(8,128)}, u32[]{:S(2)}) copy-start(f32[1,60,2048]{2,1,0:T(8,128)} %mul.939) | copy-start | bytes 1474564
  270.4 3.2 %copy-start.5 = (f32[1,60,2048]{2,1,0:T(8,128)S(1)}, f32[1,60,2048]{2,1,0:T(8,128)}, u32[]{:S(2)}) copy-start(f32[1,60,2048]{2,1,0:T(8,128)} %mul.943) | copy-start | bytes 1474564
  270.4 3.2 %copy-start.8 = (f32[1,60,2048]{2,1,0:T(8,128)S(1)}, f32[1,60,2048]{2,1,0:T(8,128)}, u32[]{:S(2)}) copy-start(f32[1,60,2048]{2,1,0:T(8,128)} %squeeze.134) | copy-start | bytes 1474564
  (5 other events, 8.9 us)
where the time goes:
time: 283 us; the launch traced here: 282 us
  local copies, waits for them, and re-layouts  164 us (58%)
  waiting for transfers between devices  50.2 us (18%)
  other arithmetic  36.3 us (13%)
  matrix products  19.4 us (7%)
  starting transfers between devices  11.1 us (4%)
    gather x2, local copies, waits for them, and re-layouts, local(): jnp.take(face_rows, send_faces, axis=0)  37.2 us
    gather x1, local copies, waits for them, and re-layouts, local(): neighbour = jnp.take(received, recv_faces, axis=0).T  30.1 us
    all_to_all x1, waiting for transfers between devices, local(): lax.all_to_all(outgoing, 'grp', split_axis=1, concat_axis=1, tiled=True)  20.6 us
    slice x4, local copies, waits for them, and re-layouts, face_flux(): jump_h = [far_split[c + 3] - own_split[c + 3] for c in range(3)]  20.5 us
    unnamed x10, other arithmetic  16.7 us
    all_to_all x1, waiting for transfers between devices, across_groups(): lax.all_to_all(outgoing, 'grp', split_axis=1, concat_axis=1, tiled=True)  15.2 us
    ppermute x2, waiting for transfers between devices, shifted(): return lax.ppermute(x, axis, [(i, (i + by) % size) for i in range(size)])  14.4 us
    dot_general x1, matrix products, volume_terms(): jnp.einsum('anm,qms->qans', deriv_mats, coefficients, precision=exact_prec)  10.5 us
  transfers between devices with their start and end apart: 4, of which 4 were waited for; matrix products, arithmetic and copies ran while one was open for 14% of the time, Pallas kernels for 0%

commit v1 on v0

v1 whole, which is shorter than its diff:
```python
import functools

import jax
import jax.numpy as jnp
from jax import lax
from jax.experimental import pallas as pl
from jax.experimental.pallas import tpu as pltpu
from jax.sharding import PartitionSpec as P

NPM = 35
FPTS = 15
COMPS = 6
FACES = 4
PP = 16
DP = 40
LANES = 128
TR = COMPS * PP
GEO = COMPS * NPM
METRIC, NORMAL, SCALE = GEO, GEO + 9, GEO + 21
ROWS = GEO + 30
BIG = 3 * DP + FACES * PP
MESH = pl.DeviceIdType.MESH
VMEM_LIMIT = 60 * 1024 * 1024


def split(x):
    high = x.astype(jnp.bfloat16)
    low = (x - high.astype(jnp.float32)).astype(jnp.bfloat16)
    return high, low


def dot3(a, b, dims):
    ah, al = a
    bh, bl = b

    def mul(x, y):
        return lax.dot_general(x, y, (dims, ((), ())), preferred_element_type=jnp.float32)

    return mul(ah, bh) + (mul(ah, bl) + mul(al, bh))


def params(**kw):
    return pltpu.CompilerParams(vmem_limit_bytes=VMEM_LIMIT, **kw)


VM = pl.BlockSpec(memory_space=pltpu.VMEM)
SM = pl.BlockSpec(memory_space=pltpu.SMEM)


def bucket_kernel(groups, cap, target_ref, fields_ref, metric_ref, normals_ref, fscale_ref, out_ref, pay):
    pay[0:GEO, :] = fields_ref[...]
    pay[METRIC : METRIC + 9, :] = metric_ref[...]
    pay[NORMAL : NORMAL + 12, :] = normals_ref[...]
    pay[SCALE : SCALE + 4, :] = fscale_ref[...]
    pay[SCALE + 4 : ROWS, :] = jnp.zeros((ROWS - SCALE - 4, pay.shape[1]), jnp.float32)
    high, low = split(pay[...])
    elements = pay.shape[1]
    target = target_ref[...]
    step = min(cap, 256)
    for g in range(groups):
        for k in range(0, cap, step):
            ids = lax.broadcasted_iota(jnp.int32, (step, elements), 0) + (g * cap + k)
            hot = jnp.where(ids == target, 1.0, 0.0).astype(jnp.bfloat16)
            dims = (((1,), (1,)), ((), ()))
            out_ref[g, :, k : k + step] = lax.dot_general(
                high, hot, dims, preferred_element_type=jnp.float32
            ) + lax.dot_general(low, hot, dims, preferred_element_type=jnp.float32)


def gather_block(index_ref, base, table, tmp):
    for i in range(LANES):
        tmp[i : i + 1, :] = table[pl.ds(index_ref[base + i], 1), :]


def send_kernel(groups, cap, lists, list_size, send_ref, bucket_ref, tt_ref, out_ref, table, tmp):
    slots = groups * cap
    weights = split(tt_ref[...])
    for g in range(groups):
        coefs = split(bucket_ref[g])
        for f in range(FACES):
            w = tuple(x[f * LANES : (f + 1) * LANES, :] for x in weights)
            table[f * slots + g * cap : f * slots + (g + 1) * cap, :] = dot3(coefs, w, ((0,), (1,)))
    table[FACES * slots : FACES * slots + 8, :] = jnp.zeros((8, LANES), jnp.float32)

    def one_list(item, _):
        for q in range(list_size // LANES):
            gather_block(send_ref, item * list_size + q * LANES, table, tmp.at[q % 2])
            out_ref[item, :, q * LANES : (q + 1) * LANES] = tmp[q % 2].T[:TR]
        return 0

    lax.fori_loop(0, lists, one_list, 0)


def exchange_kernel(groups, doms, lists_ref, out_ref, send_sem, recv_sem, local_sem):
    g = lax.axis_index("grp")
    p = lax.axis_index("dom")
    plan = [(d, j) for d in range(1, groups) for j in range(3)] + [(0, 0), (0, 2)]
    barrier = pltpu.get_barrier_semaphore()

    def peer(d, j):
        return (lax.rem(g + d, groups), lax.rem(p + j - 1 + doms, doms))

    for d, j in plan:
        pl.semaphore_signal(barrier, inc=1, device_id=peer(d, j), device_id_type=MESH)
    pl.semaphore_wait(barrier, len(plan))
    order = sorted(plan, key=lambda x: (x[0] != 2, x[0] == 0))
    copies = []
    for d, j in order:
        h = lax.rem(g + d, groups)
        copy = pltpu.make_async_remote_copy(
            src_ref=lists_ref.at[j * groups + h],
            dst_ref=out_ref.at[j * groups + g],
            send_sem=send_sem.at[d * 3 + j],
            recv_sem=recv_sem.at[d * 3 + j],
            device_id=peer(d, j),
            device_id_type=MESH,
        )
        copy.start()
        copies.append(copy)
    own = pltpu.make_async_copy(lists_ref.at[groups + g], out_ref.at[groups + g], local_sem)
    own.start()
    for d, j in order:
        src = lax.rem(g - d + groups, groups)
        pltpu.make_async_remote_copy(
            src_ref=lists_ref.at[j * groups + src],
            dst_ref=out_ref.at[j * groups + src],
            send_sem=send_sem.at[d * 3 + j],
            recv_sem=recv_sem.at[d * 3 + j],
            device_id=peer(d, j),
            device_id_type=MESH,
        ).wait_recv()
    for copy in copies:
        copy.wait_send()
    own.wait()


def cross_of(u, v):
    return [u[1] * v[2] - u[2] * v[1], u[2] * v[0] - u[0] * v[2], u[0] * v[1] - u[1] * v[0]]


CURL = ((5, 1, 4, 2), (3, 2, 5, 0), (4, 0, 3, 1), (1, 2, 2, 1), (2, 0, 0, 2), (0, 1, 1, 0))


def final_kernel(
    groups, cap, lists, list_size, recv_ref, arrived_ref, bucket_ref, tt_ref, big_ref, out_ref, table, tmp, far, flux, stack
):
    slots = groups * cap
    fill = jnp.zeros((LANES - TR, LANES), jnp.float32)

    def one_list(item, _):
        for q in range(list_size // LANES):
            block = jnp.concatenate([arrived_ref[item, :, q * LANES : (q + 1) * LANES], fill], 0)
            table[pl.ds(pl.multiple_of(item * list_size + q * LANES, LANES), LANES), :] = block.T
        return 0

    lax.fori_loop(0, lists, one_list, 0)
    table[lists * list_size : lists * list_size + 8, :] = jnp.zeros((8, LANES), jnp.float32)
    stack[...] = jnp.zeros_like(stack)
    weights = split(tt_ref[...])
    big = split(big_ref[...])

    for g in range(groups):

        def one_face(f, _):
            for q in range(cap // LANES):
                gather_block(recv_ref, f * slots + g * cap + q * LANES, table, tmp.at[q % 2])
                far[f, :, q * LANES : (q + 1) * LANES] = tmp[q % 2].T[:TR]
            return 0

        lax.fori_loop(0, FACES, one_face, 0)
        block = bucket_ref[g]
        pieces = split(block)
        for f in range(FACES):
            own = dot3(tuple(x[f * LANES : f * LANES + TR, :] for x in weights), pieces, ((1,), (0,)))
            jump = far[f] - own
            jumps = [jump[c * PP : (c + 1) * PP, :] for c in range(COMPS)]
            n = [block[NORMAL + c * FACES + f : NORMAL + c * FACES + f + 1, :] for c in range(3)]
            s = 0.5 * block[SCALE + f : SCALE + f + 1, :]
            je, jh = jumps[:3], jumps[3:]
            ne = n[0] * je[0] + n[1] * je[1] + n[2] * je[2]
            nh = n[0] * jh[0] + n[1] * jh[1] + n[2] * jh[2]
            th, te = cross_of(n, jh), cross_of(n, je)
            for c in range(3):
                flux[c, f * PP : (f + 1) * PP, :] = s * (th[c] + je[c] - n[c] * ne)
                flux[3 + c, f * PP : (f + 1) * PP, :] = s * (jh[c] - te[c] - n[c] * nh)
        coefs = [bucket_ref[g, c * NPM : (c + 1) * NPM, :] for c in range(COMPS)]
        for c in range(COMPS):
            q1, x1, q2, x2 = CURL[c]
            for a in range(3):
                m1 = block[METRIC + 3 * a + x1 : METRIC + 3 * a + x1 + 1, :]
                m2 = block[METRIC + 3 * a + x2 : METRIC + 3 * a + x2 + 1, :]
                stack[a * DP : a * DP + NPM, :] = m1 * coefs[q1] - m2 * coefs[q2]
            stack[3 * DP : BIG, :] = flux[c]
            result = dot3(big, split(stack[...]), ((1,), (0,)))
            out_ref[c * NPM : (c + 1) * NPM, g * cap : (g + 1) * cap] = result[:NPM]


def local(groups, doms, fields, metric, normals, fscale, orders, slots, send_faces, recv_faces, dmat, tmat, lmat):
    own_group = lax.axis_index("grp")
    elements = fields.shape[1]
    cap = elements // 2
    total = groups * cap
    lists = 3 * groups
    list_size = send_faces.shape[0] // lists
    f32 = jnp.float32
    target = ((orders - 1) * cap + slots).reshape(1, elements)
    outgoing = pl.pallas_call(
        functools.partial(bucket_kernel, groups, cap),
        out_shape=jax.ShapeDtypeStruct((groups, ROWS, cap), f32),
        in_specs=[VM] * 5,
        out_specs=VM,
        scratch_shapes=[pltpu.VMEM((ROWS, elements), f32)],
        compiler_params=params(),
        name="bucket",
    )(target, fields, metric, normals, fscale)
    bucket = lax.all_to_all(outgoing, "grp", split_axis=0, concat_axis=0, tiled=True)

    node_total = (own_group + 2) * (own_group + 3) * (own_group + 4) // 6
    mask = (jnp.arange(NPM, dtype=jnp.int32) < node_total).astype(f32)
    deriv = dmat[0].reshape(3, NPM, NPM) * mask[None, :, None] * mask[None, None, :]
    deriv = jnp.pad(jnp.transpose(deriv, (1, 0, 2)), ((0, 0), (0, 0), (0, DP - NPM))).reshape(NPM, 3 * DP)
    lift = jnp.transpose((lmat[0] * mask[:, None]).reshape(NPM, FPTS, FACES), (0, 2, 1))
    lift = jnp.pad(lift, ((0, 0), (0, 0), (0, PP - FPTS))).reshape(NPM, FACES * PP)
    big = jnp.pad(jnp.concatenate([deriv, lift], 1), ((0, DP - NPM), (0, 0)))
    trace = jnp.transpose((tmat[0] * mask[None, :]).reshape(FPTS, FACES, NPM), (1, 0, 2))
    trace = jnp.pad(trace, ((0, 0), (0, PP - FPTS), (0, 0)))
    wide = [
        jnp.pad(trace, ((0, 0), (0, 0), (c * NPM, ROWS - (c + 1) * NPM))) for c in range(COMPS)
    ] + [jnp.zeros((FACES, LANES - TR, ROWS), f32)]
    tt = jnp.concatenate(wide, 1).reshape(FACES * LANES, ROWS)

    outgoing_faces = pl.pallas_call(
        functools.partial(send_kernel, groups, cap, lists, list_size),
        out_shape=jax.ShapeDtypeStruct((lists, TR, list_size), f32),
        in_specs=[SM, VM, VM],
        out_specs=VM,
        scratch_shapes=[pltpu.VMEM((FACES * total + 8, LANES), f32), pltpu.VMEM((2, LANES, LANES), f32)],
        compiler_params=params(),
        name="send",
    )(send_faces, bucket, tt)
    arrived = pl.pallas_call(
        functools.partial(exchange_kernel, groups, doms),
        out_shape=jax.ShapeDtypeStruct((lists, TR, list_size), f32),
        in_specs=[VM],
        out_specs=VM,
        scratch_shapes=[
            pltpu.SemaphoreType.DMA((lists,)),
            pltpu.SemaphoreType.DMA((lists,)),
            pltpu.SemaphoreType.DMA,
        ],
        compiler_params=params(collective_id=0, has_side_effects=True),
        name="exchange",
    )(outgoing_faces)
    return pl.pallas_call(
        functools.partial(final_kernel, groups, cap, lists, list_size),
        out_shape=jax.ShapeDtypeStruct((GEO, total), f32),
        in_specs=[SM, VM, VM, VM, VM],
        out_specs=VM,
        scratch_shapes=[
            pltpu.VMEM((lists * list_size + 8, LANES), f32),
            pltpu.VMEM((2, LANES, LANES), f32),
            pltpu.VMEM((FACES, TR, cap), f32),
            pltpu.VMEM((COMPS, FACES * PP, cap), f32),
            pltpu.VMEM((BIG, cap), f32),
        ],
        compiler_params=params(),
        name="final",
    )(recv_faces, arrived, bucket, tt, big)


def solution(mesh):
    col = P(None, ("grp", "dom"))
    row = P(("grp", "dom"))
    mat = P("grp", None, None)
    in_specs = (col, col, col, col, row, row, row, row, mat, mat, mat)
    body = functools.partial(local, mesh.shape["grp"], mesh.shape["dom"])
    return jax.shard_map(body, mesh=mesh, in_specs=in_specs, out_specs=col, check_vma=False)
```

time: 283 us -> 128 us (0.45)
  local copies, waits for them, and re-layouts: 164 us -> 2.46 us
  Pallas kernels: 0 us -> 97.2 us
  other arithmetic: 36.3 us -> 2.18 us
  waiting for transfers between devices: 50.2 us -> 21 us
  matrix products: 19.4 us -> 0 us
  starting transfers between devices: 11.1 us -> 4.39 us
    pallas_call x0 -> x4, Pallas kernels: none -> 97.2 us  [the longest x1 53.7 us: local(): pl.pallas_call(functools.partial(exchange_kernel, groups, doms), out_shap...]
    gather x5 -> x0, local copies, waits for them, and re-layouts: 75.8 us -> none  [the longest x2 37.2 us: local(): jnp.take(face_rows, send_faces, axis=0)]
    slice x12 -> x0, local copies, waits for them, and re-layouts: 32.9 us -> none  [the longest x4 20.5 us: face_flux(): jump_h = [far_split[c + 3] - own_split[c + 3] for c in range(3)]]
    dot_general x3 -> x0, matrix products: 19.4 us -> none  [the longest x1 10.5 us: volume_terms(): jnp.einsum('anm,qms->qans', deriv_mats, coefficients, precision=exact_prec)]
    unnamed x10 -> x1, other arithmetic: 16.7 us -> 0.05 us
    reshape x6 -> x2, local copies, waits for them, and re-layouts: 16.2 us -> 0.17 us  [the longest x1 0.09 us: local(): jnp.pad(jnp.transpose(deriv, (1, 0, 2)), ((0, 0), (0, 0), (0, DP - NPM)))]
    all_to_all x2 -> x1, waiting for transfers between devices: 35.8 us -> 21 us  [local(): lax.all_to_all(outgoing, 'grp', split_axis=0, concat_axis=0, tiled=True)]
    ppermute x2 -> x0, waiting for transfers between devices: 14.4 us -> none  [shifted(): return lax.ppermute(x, axis, [(i, (i + by) % size) for i in range(size)])]
  transfers between devices with their start and end apart: 4 -> 1, of which waited for: 4 -> 1; matrix products, arithmetic and copies ran while one was open for 14% -> 2% of each run, Pallas kernels for 0% -> 0%
where the time goes in v1:
time: 128 us; the launch traced here: 127 us
  Pallas kernels  97.2 us (76%)
  waiting for transfers between devices  21 us (16%)
  starting transfers between devices  4.39 us (3%)
  local copies, waits for them, and re-layouts  2.46 us (2%)
  other arithmetic  2.18 us (2%)
    pallas_call x1, Pallas kernels, local(): pl.pallas_call(functools.partial(exchange_kernel, groups, doms), out_shap...  53.7 us
    pallas_call x1, Pallas kernels, local(): pl.pallas_call(functools.partial(final_kernel, groups, cap, lists, list_s...  21.8 us
    all_to_all x1, waiting for transfers between devices, local(): lax.all_to_all(outgoing, 'grp', split_axis=0, concat_axis=0, tiled=True)  21 us
    pallas_call x1, Pallas kernels, local(): pl.pallas_call(functools.partial(send_kernel, groups, cap, lists, list_si...  16.8 us
    pallas_call x1, Pallas kernels, local(): pl.pallas_call(functools.partial(bucket_kernel, groups, cap), out_shape=j...  4.89 us
    all_to_all x1, starting transfers between devices, local(): lax.all_to_all(outgoing, 'grp', split_axis=0, concat_axis=0, tiled=True)  4.39 us
  transfers between devices with their start and end apart: 1, of which 1 were waited for; matrix products, arithmetic and copies ran while one was open for 2% of the time, Pallas kernels for 0%

profile of v1, /device:TPU:1, one launch (start us, length us, event | category | flops | bytes accessed | tf_op | source)
XLA Modules:
  0.0 127.3 jit_solution(1637955016324048412)
XLA Ops:
  0.0 1.3 %multiply_add_fusion = s32[1024]{0:T(1024)} fusion(s32[1024]{0:T(1024)} %param.16, s32[1024]{0:T(1024)} %param.15), kind=kLoop, calls=%fused_computation.12 | loop fusion | flops 3072 | bytes 12288 | tf_op jit(solution)/shard_map/add | solution.py:206
  1.3 4.9 %bucket.1 = f32[4,240,512]{2,1,0:T(8,128)} custom-call(s32[1,1024]{1,0:T(1,128)} %bitcast.16, f32[210,1024]{1,0:T(8,128)} %fields_ref.1, f32[9,1024]{1,0:T(8,128)} %metric_ref.1, f32[12,1024]{1,0:T(8,128)} %normals_ref.1, f32[4,1024]{1,0:T(4,128)} %fscale_ref.1), custom_call_target="tpu_custom_call" | custom-call | tf_op jit(solution)/shard_map/bucket/pallas_call | solution.py:207
  6.2 0.0 copy-start.2
  6.2 0.0 copy-start.3
  6.2 0.0 copy-start.4
  6.2 4.4 %all-to-all-start = ((f32[4,240,512]{2,1,0:T(8,128)}), f32[4,240,512]{2,1,0:T(8,128)S(1)}, u32[]{:S(2)}, u32[]{:S(2)}) async-start(f32[4,240,512]{2,1,0:T(8,128)} %bucket.1), calls=%async_computation | async-start | bytes 3932160 | tf_op jit(solution)/shard_map/all_to_all | solution.py:216
  10.6 0.0 copy-done.2
  10.6 0.1 copy.15
  10.7 0.0 copy-done.3
  10.8 0.1 reduce
  10.8 0.1 reshape_squeeze.3
  10.9 0.1 multiply_bitcast_fusion
  11.0 0.1 copy.32
  11.2 0.1 reshape.48
  11.3 0.0 copy-done.4
  11.3 0.1 copy.23
  11.4 0.1 copy.25
  11.5 0.7 select_maximum_fusion.big_ref
  12.2 0.1 pad_dynamic-update-slice_fusion.4
  12.3 0.1 pad_dynamic-update-slice_fusion.3
  12.4 0.1 pad_dynamic-update-slice_fusion.2
  12.5 0.1 pad_dynamic-update-slice_fusion.1
  12.6 0.1 pad_dynamic-update-slice_fusion
  12.7 0.0 copy-start.1
  12.7 21.0 %all-to-all-done.bucket_ref = f32[4,240,512]{2,1,0:T(8,128)S(1)} async-done(((f32[4,240,512]{2,1,0:T(8,128)}), f32[4,240,512]{2,1,0:T(8,128)S(1)}, u32[]{:S(2)}, u32[]{:S(2)}) %all-to-all-start) | async-done | bytes 1966112 | tf_op jit(solution)/shard_map/all_to_all | solution.py:216
  33.7 0.0 copy-start
  33.7 0.0 copy-done.1
  33.7 1.4 %copy-done = f32[4,240,512]{2,1,0:T(8,128)} copy-done((f32[4,240,512]{2,1,0:T(8,128)}, f32[4,240,512]{2,1,0:T(8,128)S(1)}, u32[]{:S(2)}) %copy-start) | copy-done | bytes 1966104
  35.0 16.8 %send.1.lists_ref = f32[12,96,768]{2,1,0:T(8,128)} custom-call(s32[9216]{0:T(1024)} %send_ref.1, f32[4,240,512]{2,1,0:T(8,128)} %copy-done, f32[512,240]{1,0:T(8,128)} %bitcast.13), custom_call_target="tpu_custom_call" | custom-call | tf_op jit(solution)/shard_map/send/pallas_call | solution.py:232
  51.8 53.7 %exchange.1.arrived_ref = f32[12,96,768]{2,1,0:T(8,128)} custom-call(f32[12,96,768]{2,1,0:T(8,128)} %send.1.lists_ref), custom_call_target="tpu_custom_call" | custom-call | tf_op jit(solution)/shard_map/exchange/pallas_call | solution.py:241
  105.5 21.8 %final.1 = f32[210,2048]{1,0:T(8,128)} custom-call(s32[8192]{0:T(1024)} %recv_ref.1, f32[12,96,768]{2,1,0:T(8,128)} %exchange.1.arrived_ref, f32[4,240,512]{2,1,0:T(8,128)} %copy-done, f32[512,240]{1,0:T(8,128)} %bitcast.14, f32[40,184]{1,0:T(8,128)} %select_maximum_fusion.big_ref), custom_call_target="tpu_custom_call" | custom-call | tf_op jit(solution)/shard_map/final/pallas_call | solution.py:254
  (12 shorter events, 0.1 us)
Async XLA Ops:
  6.2 4.4 %copy-start.2 = (f32[1,60,35]{1,0,2:T(1,128)S(1)}, f32[1,60,35]{1,0,2:T(1,128)}, u32[]{:S(2)}) copy-start(f32[1,60,35]{1,0,2:T(1,128)} %param.20) | copy-start | bytes 25204
  6.2 4.6 %copy-start.3 = (f32[1,105,35]{1,0,2:T(1,128)S(1)}, f32[1,105,35]{1,0,2:T(1,128)}, u32[]{:S(2)}) copy-start(f32[1,105,35]{1,0,2:T(1,128)} %param.19) | copy-start | bytes 44104
  6.2 5.1 %copy-start.4 = (f32[1,35,60]{2,0,1:T(1,128)S(1)}, f32[1,35,60]{2,0,1:T(1,128)}, u32[]{:S(2)}) copy-start(f32[1,35,60]{2,0,1:T(1,128)} %param.21) | copy-start | bytes 25204
  6.2 27.5 %all-to-all-start = ((f32[4,240,512]{2,1,0:T(8,128)}), f32[4,240,512]{2,1,0:T(8,128)S(1)}, u32[]{:S(2)}, u32[]{:S(2)}) async-start(f32[4,240,512]{2,1,0:T(8,128)} %bucket.1), calls=%async_computation | async-start | bytes 3932160 | tf_op jit(solution)/shard_map/all_to_all | solution.py:216
  12.7 21.0 %copy-start.1 = (f32[4,128,240]{2,1,0:T(8,128)}, f32[4,128,240]{2,1,0:T(8,128)S(1)}, u32[]{:S(2)}) copy-start(f32[4,128,240]{2,1,0:T(8,128)S(1)} %broadcast_dynamic-update-slice_fusion) | copy-start | bytes 1474564
  33.7 1.4 %copy-start = (f32[4,240,512]{2,1,0:T(8,128)}, f32[4,240,512]{2,1,0:T(8,128)S(1)}, u32[]{:S(2)}) copy-start(f32[4,240,512]{2,1,0:T(8,128)S(1)} %all-to-all-done.bucket_ref) | copy-start | bytes 5898244

commit v2 on v1

v2 whole, which is shorter than its diff:
```python
import functools

import jax
import jax.numpy as jnp
from jax import lax
from jax.experimental import pallas as pl
from jax.experimental.pallas import tpu as pltpu
from jax.sharding import PartitionSpec as P

NPM = 35
FPTS = 15
COMPS = 6
FACES = 4
PP = 16
DP = 40
LANES = 128
TR = COMPS * PP
GEO = COMPS * NPM
METRIC, NORMAL, SCALE = GEO, GEO + 9, GEO + 21
ROWS = GEO + 30
BIG = 3 * DP + FACES * PP
MESH = pl.DeviceIdType.MESH
VMEM_LIMIT = 32 * 1024 * 1024


def split(x):
    high = x.astype(jnp.bfloat16)
    low = (x - high.astype(jnp.float32)).astype(jnp.bfloat16)
    return high, low


def dot3(a, b, dims):
    ah, al = a
    bh, bl = b

    def mul(x, y):
        return lax.dot_general(x, y, (dims, ((), ())), preferred_element_type=jnp.float32)

    return mul(ah, bh) + (mul(ah, bl) + mul(al, bh))


def params(**kw):
    return pltpu.CompilerParams(vmem_limit_bytes=VMEM_LIMIT, **kw)


VM = pl.BlockSpec(memory_space=pltpu.VMEM)
SM = pl.BlockSpec(memory_space=pltpu.SMEM)


def partner(g, d, groups):
    if groups & (groups - 1):
        return lax.rem(g + d, groups)
    other = g
    bit = 1
    while bit <= d:
        if d & bit:
            other = other + bit - 2 * bit * lax.rem(g // bit, 2)
        bit *= 2
    return other


def source(g, d, groups):
    if groups & (groups - 1):
        return lax.rem(g - d + groups, groups)
    return partner(g, d, groups)


def bucket_kernel(
    groups, cap, target_ref, fields_ref, metric_ref, normals_ref, fscale_ref, out_ref, pay, sbuf, send_sem, recv_sem
):
    g = lax.axis_index("grp")
    p = lax.axis_index("dom")
    barrier = pltpu.get_barrier_semaphore()
    for d in range(1, groups):
        pl.semaphore_signal(barrier, inc=1, device_id=(partner(g, d, groups), p), device_id_type=MESH)
    pay[0:GEO, :] = fields_ref[...]
    pay[METRIC : METRIC + 9, :] = metric_ref[...]
    pay[NORMAL : NORMAL + 12, :] = normals_ref[...]
    pay[SCALE : SCALE + 4, :] = fscale_ref[...]
    pay[SCALE + 4 : ROWS, :] = jnp.zeros((ROWS - SCALE - 4, pay.shape[1]), jnp.float32)
    high, low = split(pay[...])
    elements = pay.shape[1]
    target = target_ref[...]
    step = min(cap, 256)
    dims = (((1,), (1,)), ((), ()))

    def build(h, dst):
        for k in range(0, cap, step):
            ids = lax.broadcasted_iota(jnp.int32, (step, elements), 0) + (h * cap + k)
            hot = jnp.where(ids == target, 1.0, 0.0).astype(jnp.bfloat16)
            dst[:, k : k + step] = lax.dot_general(
                high, hot, dims, preferred_element_type=jnp.float32
            ) + lax.dot_general(low, hot, dims, preferred_element_type=jnp.float32)

    copies = [
        pltpu.make_async_remote_copy(
            src_ref=sbuf.at[d - 1],
            dst_ref=out_ref.at[g],
            send_sem=send_sem.at[d - 1],
            recv_sem=recv_sem.at[d - 1],
            device_id=(partner(g, d, groups), p),
            device_id_type=MESH,
        )
        for d in range(1, groups)
    ]
    build(partner(g, 1, groups), sbuf.at[0])
    pl.semaphore_wait(barrier, groups - 1)
    for d in range(2, groups):
        build(partner(g, d, groups), sbuf.at[d - 1])
        copies[d - 2].start()
    build(g, out_ref.at[g])
    copies[groups - 2].start()
    for d in range(1, groups):
        src = source(g, d, groups)
        pltpu.make_async_remote_copy(
            src_ref=sbuf.at[d - 1],
            dst_ref=out_ref.at[src],
            send_sem=send_sem.at[d - 1],
            recv_sem=recv_sem.at[d - 1],
            device_id=(partner(g, d, groups), p),
            device_id_type=MESH,
        ).wait_recv()
    for copy in copies:
        copy.wait_send()


def gather_block(index_ref, base, table, tmp):
    for i in range(LANES):
        tmp[i : i + 1, :] = table[pl.ds(index_ref[base + i], 1), :]


def exchange_kernel(
    groups, doms, cap, list_size, send_ref, bucket_ref, tt_ref, out_ref, table, tmp, sbuf, arrived, send_sem, recv_sem
):
    g = lax.axis_index("grp")
    p = lax.axis_index("dom")
    slots = groups * cap
    blocks = list_size // LANES
    lists = 3 * groups
    plan = [(d, j) for j in (2, 0, 1) for d in (1, 2, 0) if (d, j) != (0, 1) and d < groups]
    plan += [(d, j) for d in range(3, groups) for j in (2, 0, 1)]
    barrier = pltpu.get_barrier_semaphore()

    def peer(d, j):
        return (partner(g, d, groups), lax.rem(p + j - 1 + doms, doms))

    for d, j in plan:
        pl.semaphore_signal(barrier, inc=1, device_id=peer(d, j), device_id_type=MESH)

    weights = split(tt_ref[...])
    for b in range(groups):
        coefs = split(bucket_ref[b])
        for f in range(FACES):
            w = tuple(x[f * LANES : (f + 1) * LANES, :] for x in weights)
            table[f * slots + b * cap : f * slots + (b + 1) * cap, :] = dot3(coefs, w, ((0,), (1,)))
    table[FACES * slots : FACES * slots + 8, :] = jnp.zeros((8, LANES), jnp.float32)
    pl.semaphore_wait(barrier, len(plan))

    copies = []
    for n, (d, j) in enumerate(plan):
        base = (j * groups + partner(g, d, groups)) * list_size

        def pair(i, _, n=n, base=base):
            for k in range(2):
                at = pl.multiple_of((2 * i + k) * LANES, LANES)
                gather_block(send_ref, base + at, table, tmp.at[k])
                sbuf[n, :, pl.ds(at, LANES)] = tmp[k].T[:TR]
            return 0

        lax.fori_loop(0, blocks // 2, pair, 0)
        copies.append(
            pltpu.make_async_remote_copy(
                src_ref=sbuf.at[n],
                dst_ref=arrived.at[n],
                send_sem=send_sem.at[n],
                recv_sem=recv_sem.at[n],
                device_id=peer(d, j),
                device_id_type=MESH,
            )
        )
        if n:
            copies[n - 1].start()

    own = (groups + g) * list_size

    def own_block(i, _):
        at = pl.multiple_of(own + i * LANES, LANES)
        gather_block(send_ref, at, table, tmp.at[0])
        out_ref[pl.ds(at, LANES), :] = tmp[0]
        return 0

    lax.fori_loop(0, blocks, own_block, 0)
    copies[-1].start()
    out_ref[lists * list_size : lists * list_size + 8, :] = jnp.zeros((8, LANES), jnp.float32)
    fill = jnp.zeros((LANES - TR, LANES), jnp.float32)
    for n, (d, j) in enumerate(plan):
        copies[n].wait_recv()
        base = (j * groups + source(g, d, groups)) * list_size
        for q in range(blocks):
            block = jnp.concatenate([arrived[n, :, q * LANES : (q + 1) * LANES], fill], 0)
            out_ref[pl.ds(pl.multiple_of(base + q * LANES, LANES), LANES), :] = block.T
    for copy in copies:
        copy.wait_send()


def cross_of(u, v):
    return [u[1] * v[2] - u[2] * v[1], u[2] * v[0] - u[0] * v[2], u[0] * v[1] - u[1] * v[0]]


CURL = ((5, 1, 4, 2), (3, 2, 5, 0), (4, 0, 3, 1), (1, 2, 2, 1), (2, 0, 0, 2), (0, 1, 1, 0))


def final_kernel(
    groups, cap, recv_ref, table, bucket_ref, tt_ref, big_ref, out_ref, tmp, far, flux, stack
):
    slots = groups * cap
    stack[...] = jnp.zeros_like(stack)
    weights = split(tt_ref[...])
    big = split(big_ref[...])

    for g in range(groups):

        def one_face(f, _):
            for q in range(cap // LANES):
                gather_block(recv_ref, f * slots + g * cap + q * LANES, table, tmp.at[q % 2])
                far[f, :, q * LANES : (q + 1) * LANES] = tmp[q % 2].T[:TR]
            return 0

        lax.fori_loop(0, FACES, one_face, 0)
        block = bucket_ref[g]
        pieces = split(block)
        for f in range(FACES):
            own = dot3(tuple(x[f * LANES : f * LANES + TR, :] for x in weights), pieces, ((1,), (0,)))
            jump = far[f] - own
            jumps = [jump[c * PP : (c + 1) * PP, :] for c in range(COMPS)]
            n = [block[NORMAL + c * FACES + f : NORMAL + c * FACES + f + 1, :] for c in range(3)]
            s = 0.5 * block[SCALE + f : SCALE + f + 1, :]
            je, jh = jumps[:3], jumps[3:]
            ne = n[0] * je[0] + n[1] * je[1] + n[2] * je[2]
            nh = n[0] * jh[0] + n[1] * jh[1] + n[2] * jh[2]
            th, te = cross_of(n, jh), cross_of(n, je)
            for c in range(3):
                flux[c, f * PP : (f + 1) * PP, :] = s * (th[c] + je[c] - n[c] * ne)
                flux[3 + c, f * PP : (f + 1) * PP, :] = s * (jh[c] - te[c] - n[c] * nh)
        coefs = [bucket_ref[g, c * NPM : (c + 1) * NPM, :] for c in range(COMPS)]
        for c in range(COMPS):
            q1, x1, q2, x2 = CURL[c]
            for a in range(3):
                m1 = block[METRIC + 3 * a + x1 : METRIC + 3 * a + x1 + 1, :]
                m2 = block[METRIC + 3 * a + x2 : METRIC + 3 * a + x2 + 1, :]
                stack[a * DP : a * DP + NPM, :] = m1 * coefs[q1] - m2 * coefs[q2]
            stack[3 * DP : BIG, :] = flux[c]
            result = dot3(big, split(stack[...]), ((1,), (0,)))
            out_ref[c * NPM : (c + 1) * NPM, g * cap : (g + 1) * cap] = result[:NPM]


def local(groups, doms, fields, metric, normals, fscale, orders, slots, send_faces, recv_faces, dmat, tmat, lmat):
    own_group = lax.axis_index("grp")
    elements = fields.shape[1]
    cap = elements // 2
    total = groups * cap
    lists = 3 * groups
    list_size = send_faces.shape[0] // lists
    f32 = jnp.float32
    target = ((orders - 1) * cap + slots).reshape(1, elements)
    bucket = pl.pallas_call(
        functools.partial(bucket_kernel, groups, cap),
        out_shape=jax.ShapeDtypeStruct((groups, ROWS, cap), f32),
        in_specs=[VM] * 5,
        out_specs=VM,
        scratch_shapes=[
            pltpu.VMEM((ROWS, elements), f32),
            pltpu.VMEM((groups - 1, ROWS, cap), f32),
            pltpu.SemaphoreType.DMA((groups - 1,)),
            pltpu.SemaphoreType.DMA((groups - 1,)),
        ],
        compiler_params=params(collective_id=1, has_side_effects=True),
        name="bucket",
    )(target, fields, metric, normals, fscale)

    node_total = (own_group + 2) * (own_group + 3) * (own_group + 4) // 6
    mask = (jnp.arange(NPM, dtype=jnp.int32) < node_total).astype(f32)
    deriv = dmat[0].reshape(3, NPM, NPM) * mask[None, :, None] * mask[None, None, :]
    deriv = jnp.pad(jnp.transpose(deriv, (1, 0, 2)), ((0, 0), (0, 0), (0, DP - NPM))).reshape(NPM, 3 * DP)
    lift = jnp.transpose((lmat[0] * mask[:, None]).reshape(NPM, FPTS, FACES), (0, 2, 1))
    lift = jnp.pad(lift, ((0, 0), (0, 0), (0, PP - FPTS))).reshape(NPM, FACES * PP)
    big = jnp.pad(jnp.concatenate([deriv, lift], 1), ((0, DP - NPM), (0, 0)))
    trace = jnp.transpose((tmat[0] * mask[None, :]).reshape(FPTS, FACES, NPM), (1, 0, 2))
    trace = jnp.pad(trace, ((0, 0), (0, PP - FPTS), (0, 0)))
    wide = [
        jnp.pad(trace, ((0, 0), (0, 0), (c * NPM, ROWS - (c + 1) * NPM))) for c in range(COMPS)
    ] + [jnp.zeros((FACES, LANES - TR, ROWS), f32)]
    tt = jnp.concatenate(wide, 1).reshape(FACES * LANES, ROWS)

    received = pl.pallas_call(
        functools.partial(exchange_kernel, groups, doms, cap, list_size),
        out_shape=jax.ShapeDtypeStruct((lists * list_size + 8, LANES), f32),
        in_specs=[SM, VM, VM],
        out_specs=VM,
        scratch_shapes=[
            pltpu.VMEM((FACES * total + 8, LANES), f32),
            pltpu.VMEM((2, LANES, LANES), f32),
            pltpu.VMEM((lists - 1, TR, list_size), f32),
            pltpu.VMEM((lists - 1, TR, list_size), f32),
            pltpu.SemaphoreType.DMA((lists - 1,)),
            pltpu.SemaphoreType.DMA((lists - 1,)),
        ],
        compiler_params=params(collective_id=0, has_side_effects=True),
        name="exchange",
    )(send_faces, bucket, tt)
    return pl.pallas_call(
        functools.partial(final_kernel, groups, cap),
        out_shape=jax.ShapeDtypeStruct((GEO, total), f32),
        in_specs=[SM, VM, VM, VM, VM],
        out_specs=VM,
        scratch_shapes=[
            pltpu.VMEM((2, LANES, LANES), f32),
            pltpu.VMEM((FACES, TR, cap), f32),
            pltpu.VMEM((COMPS, FACES * PP, cap), f32),
            pltpu.VMEM((BIG, cap), f32),
        ],
        compiler_params=params(),
        name="final",
    )(recv_faces, received, bucket, tt, big)


def solution(mesh):
    col = P(None, ("grp", "dom"))
    row = P(("grp", "dom"))
    mat = P("grp", None, None)
    in_specs = (col, col, col, col, row, row, row, row, mat, mat, mat)
    body = functools.partial(local, mesh.shape["grp"], mesh.shape["dom"])
    return jax.shard_map(body, mesh=mesh, in_specs=in_specs, out_specs=col, check_vma=False)
```

time: 128 us -> 99.8 us (0.78)
  waiting for transfers between devices: 21 us -> 0 us
  starting transfers between devices: 4.39 us -> 0 us
  Pallas kernels: 97.2 us -> 95 us
    pallas_call x3 -> x2, Pallas kernels: 92.3 us -> 68.5 us  [the longest x1 50.1 us: local(): pl.pallas_call(functools.partial(exchange_kernel, groups, doms, cap, list...]
    pallas_call x1, Pallas kernels: 4.89 us -> 26.5 us  [local(): pl.pallas_call(functools.partial(bucket_kernel, groups, cap), out_shape=j...]
    all_to_all x1 -> x0, waiting for transfers between devices: 21 us -> none  [local(): lax.all_to_all(outgoing, 'grp', split_axis=0, concat_axis=0, tiled=True)]
    all_to_all x1 -> x0, starting transfers between devices: 4.39 us -> none  [local(): lax.all_to_all(outgoing, 'grp', split_axis=0, concat_axis=0, tiled=True)]
  transfers between devices with their start and end apart: 1 -> 0, of which waited for: 1 -> 0; matrix products, arithmetic and copies ran while one was open for 2% -> 0% of each run, Pallas kernels for 0% -> 0%
where the time goes in v2:
time: 99.8 us; the launch traced here: 99.5 us
  Pallas kernels  95 us (95%)
  local copies, waits for them, and re-layouts  2.56 us (3%)
  other arithmetic  1.77 us (2%)
    pallas_call x1, Pallas kernels, local(): pl.pallas_call(functools.partial(exchange_kernel, groups, doms, cap, list...  50.1 us
    pallas_call x1, Pallas kernels, local(): pl.pallas_call(functools.partial(bucket_kernel, groups, cap), out_shape=j...  26.5 us
    pallas_call x1, Pallas kernels, local(): pl.pallas_call(functools.partial(final_kernel, groups, cap), out_shape=ja...  18.3 us
    unnamed x23, local copies, waits for them, and re-layouts  2.21 us

profile of v2, /device:TPU:1, one launch (start us, length us, event | category | flops | bytes accessed | tf_op | source)
XLA Modules:
  0.0 99.5 jit_solution(1393509755707222629)
XLA Ops:
  0.0 0.0 copy-start.5
  0.0 0.0 copy-start.2
  0.0 0.0 copy-start.1
  0.0 0.0 copy-start
  0.0 0.8 multiply_add_fusion
  0.8 0.8 reduce
  1.6 0.8 copy.15
  2.5 0.8 copy.23
  3.4 0.1 copy.25
  3.5 0.1 reshape_squeeze.3
  3.6 0.1 multiply_bitcast_fusion
  3.7 0.1 copy.32
  3.8 0.0 copy-start.3
  3.8 0.1 reshape.48
  3.9 0.1 select_maximum_fusion.big_ref
  4.0 0.1 pad_dynamic-update-slice_fusion.4
  4.1 0.1 pad_dynamic-update-slice_fusion.3
  4.2 0.1 pad_dynamic-update-slice_fusion.2
  4.3 0.1 pad_dynamic-update-slice_fusion.1
  4.4 0.1 pad_dynamic-update-slice_fusion
  4.5 0.0 copy-done.5
  4.5 0.0 copy-done.2
  4.5 0.0 copy-done.1
  4.5 0.0 copy-done
  4.5 26.5 %bucket.1.bucket_ref = f32[4,240,512]{2,1,0:T(8,128)S(1)} custom-call(s32[1,1024]{1,0:T(1,128)S(1)} %bitcast.15, f32[210,1024]{1,0:T(8,128)S(1)} %copy-done, f32[9,1024]{1,0:T(8,128)S(1)} %copy-done.1, f32[12,1024]{1,0:T(8,128)S(1)} %copy-done.2, f32[4,1024]{1,0:T(4,128)S(1)} %copy-done.5), custom_call_target="tpu_custom_call" | custom-call | tf_op jit(solution)/shard_map/bucket/pallas_call | solution.py:266
  31.0 0.0 copy-done.3
  31.0 0.0 copy-start.4
  31.0 50.1 %exchange.1.table = f32[9224,128]{1,0:T(8,128)S(1)} custom-call(s32[9216]{0:T(1024)S(1)} %copy-done.3, f32[4,240,512]{2,1,0:T(8,128)S(1)} %bucket.1.bucket_ref, f32[512,240]{1,0:T(8,128)S(1)} %bitcast.13), custom_call_target="tpu_custom_call" | custom-call | tf_op jit(solution)/shard_map/exchange/pallas_call | solution.py:295
  81.2 0.0 copy-done.4
  81.2 18.3 %final.1 = f32[210,2048]{1,0:T(8,128)} custom-call(s32[8192]{0:T(1024)S(1)} %copy-done.4, f32[9224,128]{1,0:T(8,128)S(1)} %exchange.1.table, f32[4,240,512]{2,1,0:T(8,128)S(1)} %bucket.1.bucket_ref, f32[512,240]{1,0:T(8,128)S(1)} %bitcast.14, f32[40,184]{1,0:T(8,128)S(1)} %select_maximum_fusion.big_ref), custom_call_target="tpu_custom_call" | custom-call | tf_op jit(solution)/shard_map/final/pallas_call | solution.py:311
  (12 shorter events, 0.1 us)
Async XLA Ops:
  0.0 4.5 %copy-start.5 = (f32[4,1024]{1,0:T(4,128)S(1)}, f32[4,1024]{1,0:T(4,128)}, u32[]{:S(2)}) copy-start(f32[4,1024]{1,0:T(4,128)} %fscale_ref.1) | copy-start | bytes 49156
  0.0 4.5 %copy-start.2 = (f32[12,1024]{1,0:T(8,128)S(1)}, f32[12,1024]{1,0:T(8,128)}, u32[]{:S(2)}) copy-start(f32[12,1024]{1,0:T(8,128)} %normals_ref.1) | copy-start | bytes 147460
  0.0 4.5 %copy-start.1 = (f32[9,1024]{1,0:T(8,128)S(1)}, f32[9,1024]{1,0:T(8,128)}, u32[]{:S(2)}) copy-start(f32[9,1024]{1,0:T(8,128)} %metric_ref.1) | copy-start | bytes 110596
  0.0 4.5 %copy-start = (f32[210,1024]{1,0:T(8,128)S(1)}, f32[210,1024]{1,0:T(8,128)}, u32[]{:S(2)}) copy-start(f32[210,1024]{1,0:T(8,128)} %fields_ref.1) | copy-start | bytes 2580484
  3.8 27.2 %copy-start.3 = (s32[9216]{0:T(1024)S(1)}, s32[9216]{0:T(1024)}, u32[]{:S(2)}) copy-start(s32[9216]{0:T(1024)} %send_ref.1) | copy-start | bytes 110596
  31.0 50.2 %copy-start.4 = (s32[8192]{0:T(1024)S(1)}, s32[8192]{0:T(1024)}, u32[]{:S(2)}) copy-start(s32[8192]{0:T(1024)} %recv_ref.1) | copy-start | bytes 98308
